TPU v7x, 32 devices: a whole 2x2x4 slice. The times are simulated.
32 devices in a mesh: gx: 8 (over z, y), gy: 4 (over x, core).
Axes of the slice: x: 2, y: 2, z: 4, core: 2. Of those that a mesh axis runs over, the one named last changes fastest.
Arguments:
- basis: bfloat16 [40960, 120], P(('gx', 'gy')), may hold values from -0.03125 to 0.03125
- snapshots: bfloat16 [40960, 256], P(('gx', 'gy')), may hold values from -6 to 6
- derivatives: bfloat16 [40960, 256], P(('gx', 'gy')), may hold values from -24 to 24
- quad_pairs: int32 [2, 7260], replicated, may hold values from 0 to 119, as said below
- penalty: float32 [7381], replicated, may hold values from 0.5 to 8
Outputs:
- operator: float32 [120, 7381], replicated
Inputs may be any that keep to these rules, and one draw needn't show every extreme that they name: `quad_pairs`: every pair (i, j) with 0 <= i <= j < 120 stands in exactly one column, in an order drawn from the seed.
All inputs are finite; a program needn't handle non-finite values.
Results may differ from a plain program's by a relative error of at most 0.0003.
Values sent between devices are 32-bit elements; how exact they have to be, the bound alone decides.
A program may use at most 64 MiB of HBM per device.

v0:
```python
import functools
import math

import jax
import jax.numpy as jnp
from jax import lax
from jax.experimental import pallas as pl
from jax.experimental.pallas import tpu as pltpu
from jax.sharding import PartitionSpec as P

MESH = pl.DeviceIdType.MESH
LANES = 128
TILE = 256
highest = lax.Precision.HIGHEST
VM = pl.BlockSpec(memory_space=pltpu.VMEM)


def dot(a, b, ca, cb, precision=None):
    return lax.dot_general(
        a, b, (((ca,), (cb,)), ((), ())), precision=precision, preferred_element_type=jnp.float32
    )


def reduce_kernel(gx, gy, basis_ref, snap_ref, deriv_ref, out_ref, part, recv, send1, recv1, send2, recv2):
    n = gx * gy
    me = lax.axis_index("gx") * gy + lax.axis_index("gy")
    order = basis_ref.shape[1]
    rows = part.shape[1]

    def where(k):
        other = lax.rem(me + k, n)
        return other, (other // gy, lax.rem(other, gy))

    barrier = pltpu.get_barrier_semaphore()

    def greet(k, c):
        _, at = where(k)
        pl.semaphore_signal(barrier, inc=1, device_id=at, device_id_type=MESH)
        return c

    lax.fori_loop(1, n, greet, 0)
    basis = basis_ref[...]
    padded = rows * n // 2
    for which, ref in enumerate((snap_ref, deriv_ref)):
        prod = dot(basis, ref[...], 0, 0)
        prod = jnp.concatenate([prod, jnp.zeros((padded - order, prod.shape[1]), jnp.float32)], axis=0)
        part[which * (n // 2):(which + 1) * (n // 2)] = prod.reshape(n // 2, rows, prod.shape[1])
    pl.semaphore_wait(barrier, n - 1)

    def scatter(k):
        other, at = where(k)
        return pltpu.make_async_remote_copy(
            src_ref=part.at[other], dst_ref=recv.at[me], send_sem=send1.at[k], recv_sem=recv1.at[k],
            device_id=at, device_id_type=MESH)

    def spread(k):
        _, at = where(k)
        return pltpu.make_async_remote_copy(
            src_ref=recv.at[me], dst_ref=out_ref.at[me], send_sem=send2.at[k], recv_sem=recv2.at[k],
            device_id=at, device_id_type=MESH)

    def start(make):
        def go(k, c):
            make(k).start()
            return c
        lax.fori_loop(1, n, go, 0)

    def finish(make):
        def go(k, c):
            make(k).wait()
            return c
        lax.fori_loop(1, n, go, 0)

    start(scatter)
    recv[me] = part[me]
    finish(scatter)

    def add(k, total):
        return total + recv[k]

    total = lax.fori_loop(0, n, add, jnp.zeros(recv.shape[1:], jnp.float32))
    recv[me] = total
    start(spread)
    out_ref[me] = total
    finish(spread)


def fit_kernel(order, ones_row, cr_ref, pairs_ref, pen_ref, out_ref, t_ref, w_ref, x_ref, sem):
    snaps = cr_ref.shape[1]
    half = cr_ref.shape[0] // 2
    padded = t_ref.shape[1]
    width = x_ref.shape[1]
    coeffs = cr_ref[0:half]
    g = cr_ref[half:half + order] * (1.0 / math.sqrt(snaps))
    sq = coeffs * coeffs
    ct = coeffs.T
    inner = dot(ct, coeffs, 1, 0, highest)
    inner2 = dot(sq.T, sq, 1, 0, highest)
    kernel = 1.0 + inner + 0.5 * (inner * inner + inner2)
    s1 = dot(g, kernel, 1, 0, highest)
    ks1 = dot(s1, kernel, 1, 0, highest) * (1.0 / snaps)
    lhs = jnp.concatenate([g, s1 * (1.0 / snaps)], axis=0)
    lhs_hi = lhs.astype(jnp.bfloat16)
    lhs_lo = (lhs - lhs_hi.astype(jnp.float32)).astype(jnp.bfloat16)
    lhs_both = jnp.concatenate([lhs_hi, lhs_lo], axis=0)
    table = jnp.where(lax.broadcasted_iota(jnp.int32, ct.shape, 1) == ones_row, 1.0, ct)

    def tile(at, carry):
        dpt, tt, tw = carry
        base = pl.multiple_of(at * TILE, TILE)
        cols = []
        for h in range(TILE // LANES):
            sl = pl.ds(pl.multiple_of(base + h * LANES, LANES), LANES)
            left = jnp.take_along_axis(
                table, jnp.broadcast_to(pairs_ref[0:1, sl], table.shape), axis=1, mode="promise_in_bounds")
            right = jnp.take_along_axis(
                table, jnp.broadcast_to(pairs_ref[1:2, sl], table.shape), axis=1, mode="promise_in_bounds")
            cols.append(left * right)
        d = jnp.concatenate(cols, axis=1)
        d_hi = d.astype(jnp.bfloat16)
        d_lo = (d - d_hi.astype(jnp.float32)).astype(jnp.bfloat16)
        both = dot(lhs_both, d_hi, 1, 0)
        tv = both[:2 * order] + both[2 * order:] + dot(lhs_hi, d_lo, 1, 0)
        t, v = tv[:order], tv[order:]
        sl = pl.ds(base, TILE)
        pt = pen_ref[0:1, sl] * t
        w = v + pt
        t_ref[:, sl] = t
        w_ref[:, sl] = w
        dpt = dpt + dot(d_hi, pt.astype(jnp.bfloat16), 1, 1)
        sq, cross = t * t, t * w
        for h in range(TILE // LANES):
            tt = tt + sq[:, h * LANES:(h + 1) * LANES]
            tw = tw + cross[:, h * LANES:(h + 1) * LANES]
        return dpt, tt, tw

    zero = jnp.zeros((order, LANES), jnp.float32)
    dpt, tt, tw = lax.fori_loop(
        0, padded // TILE, tile, (jnp.zeros((snaps, order), jnp.float32), zero, zero))
    tt = jnp.sum(tt, axis=1, keepdims=True)
    tw = jnp.sum(tw, axis=1, keepdims=True)
    alpha = tt / tw
    image = ks1 + jnp.pad(dpt, ((0, 0), (0, LANES - order))).T[:order]
    moved = s1 - alpha * image
    gram = jnp.sum(moved * moved, axis=1, keepdims=True) * (1.0 / snaps)
    group = 8 * max(d for d in range(1, 6) if order // 8 % d == 0)
    copies = []
    for at in range(0, order, group):
        rows = slice(at, at + group)
        a = alpha[rows]
        t, w = t_ref[rows, :], w_ref[rows, :]
        r = t - a * w
        rr = r * r
        weighted = jnp.sum(rr * pen_ref[0:1, :], axis=1, keepdims=True) + gram[rows]
        now = jnp.sum(rr, axis=1, keepdims=True)
        ratio = now / tt[rows]
        second = now / (weighted - ratio * now / a)
        x = (a + second * ratio) * t + second * r
        x_ref[rows, :] = x[:, :width]
        copy = pltpu.make_async_copy(x_ref.at[rows, :], out_ref.at[rows, :], sem.at[at // group])
        copy.start()
        copies.append(copy)
    for copy in copies:
        copy.wait()


def solution(mesh):
    gx, gy = mesh.shape["gx"], mesh.shape["gy"]
    n = gx * gy

    def on_device(basis, snapshots, derivatives, quad_pairs, penalty):
        order, snaps = basis.shape[1], snapshots.shape[1]
        count = quad_pairs.shape[1]
        width = 1 + order + count
        padded = -(-width // TILE) * TILE
        half = LANES
        rows = 2 * half // n
        f32 = jnp.float32
        total = pl.pallas_call(
            functools.partial(reduce_kernel, gx, gy),
            out_shape=jax.ShapeDtypeStruct((n, rows, snaps), f32),
            in_specs=[VM] * 3,
            out_specs=VM,
            scratch_shapes=[pltpu.VMEM((n, rows, snaps), f32)] * 2 + [pltpu.SemaphoreType.DMA((n,))] * 4,
            compiler_params=pltpu.CompilerParams(collective_id=0, has_side_effects=True),
            name="reduce",
        )(basis, snapshots, derivatives)
        linear = jnp.arange(order, dtype=jnp.int32)
        one = jnp.full((1,), order, jnp.int32)
        ones = jnp.full((order,), order, jnp.int32)
        tail = jnp.full((padded - width,), LANES - 1, jnp.int32)
        pairs = jnp.stack([
            jnp.concatenate([one, linear, quad_pairs[0], tail]),
            jnp.concatenate([one, ones, quad_pairs[1], tail]),
        ])
        weights = jnp.pad(penalty, (0, padded - width))[None, :]
        return pl.pallas_call(
            functools.partial(fit_kernel, order, order),
            out_shape=jax.ShapeDtypeStruct((order, width), f32),
            in_specs=[VM] * 3,
            out_specs=pl.BlockSpec(memory_space=pl.ANY),
            scratch_shapes=[
                pltpu.VMEM((order, padded), f32),
                pltpu.VMEM((order, padded), f32),
                pltpu.VMEM((order, width), f32),
                pltpu.SemaphoreType.DMA((order // 8,)),
            ],
            compiler_params=pltpu.CompilerParams(vmem_limit_bytes=48 * 1024 * 1024),
            name="fit",
        )(total.reshape(n * rows, snaps), pairs, weights)

    in_specs = (P(("gx", "gy"), None), P(("gx", "gy"), None), P(("gx", "gy"), None), P(), P())
    return jax.shard_map(on_device, mesh=mesh, in_specs=in_specs, out_specs=P(), check_vma=False)
```

profile of v0, /device:TPU:0, one launch (start us, length us, event | category | flops | bytes accessed | tf_op | source)
XLA Modules:
  0.0 57.2 jit_solution(7229329244204193076)
XLA Ops:
  0.0 0.8 %pad.4 = f32[7424]{0:T(1024)S(1)} pad(f32[7381]{0:T(1024)} %param.9, f32[]{:T(128)} %constant.8.clone.1), padding=0_43 | pad | bytes 59224 | tf_op jit(solution)/shard_map/jit(_pad)/pad | solution.py:196
  0.8 1.0 %slice_reduce_fusion.1 = (s32[7260]{0:T(1024)S(1)}, s32[7260]{0:T(1024)S(1)}) fusion(s32[2,7260]{1,0:T(2,128)} %param.8), kind=kLoop, calls=%fused_computation.2 | loop fusion | bytes 116160 | tf_op jit(solution)/shard_map/slice | solution.py:193
  1.8 0.1 concatenate.6
  2.0 0.1 concatenate.7
  2.1 0.1 pad_add_fusion.pairs_ref
  2.2 1.9 %copy.6.basis_ref = bf16[1280,120]{1,0:T(8,128)(2,1)} copy(bf16[1280,120]{0,1:T(8,128)(2,1)} %param.5) | data formatting | bytes 614400 | tf_op args[0]
  4.0 23.7 %reduce.5 = f32[32,8,256]{2,1,0:T(8,128)} custom-call(bf16[1280,120]{1,0:T(8,128)(2,1)} %copy.6.basis_ref, bf16[1280,256]{1,0:T(8,128)(2,1)} %snap_ref.1, bf16[1280,256]{1,0:T(8,128)(2,1)} %deriv_ref.1), custom_call_target="tpu_custom_call" | custom-call | tf_op jit(solution)/shard_map/reduce/pallas_call | solution.py:179
  27.7 0.0 copy-start
  27.7 0.9 %copy-done = f32[32,8,256]{2,1,0:T(8,128)S(1)} copy-done((f32[32,8,256]{2,1,0:T(8,128)S(1)}, f32[32,8,256]{2,1,0:T(8,128)}, u32[]{:S(2)}) %copy-start) | copy-done | bytes 262168
  28.7 28.6 %fit.1 = f32[120,7381]{1,0:T(8,128)} custom-call(f32[256,256]{1,0:T(8,128)S(1)} %bitcast.1, s32[2,7424]{1,0:T(2,128)S(1)} %pad_add_fusion.pairs_ref, f32[1,7424]{1,0:T(1,128)S(1)} %broadcast_in_dim.11.pen_ref), custom_call_target="tpu_custom_call" | custom-call | tf_op jit(solution)/shard_map/fit/pallas_call | solution.py:197
  (6 shorter events, 0.1 us)
Async XLA Ops:
  27.7 1.0 %copy-start = (f32[32,8,256]{2,1,0:T(8,128)S(1)}, f32[32,8,256]{2,1,0:T(8,128)}, u32[]{:S(2)}) copy-start(f32[32,8,256]{2,1,0:T(8,128)} %reduce.5) | copy-start | bytes 786436
where the time goes:
time: 57.6 us; the launch traced here: 57.2 us
  Pallas kernels  52.2 us (91%)
  local copies, waits for them, and re-layouts  4.86 us (8%)
    pallas_call x1, Pallas kernels, on_device(): pl.pallas_call(functools.partial(fit_kernel, order, order), out_shape=jax...  28.6 us
    pallas_call x1, Pallas kernels, on_device(): pl.pallas_call(functools.partial(reduce_kernel, gx, gy), out_shape=jax.Sh...  23.7 us
    unnamed x3, local copies, waits for them, and re-layouts  2.81 us

commit v1 on v0

v1 whole, which is shorter than its diff:
```python
import functools
import math

import jax
import jax.numpy as jnp
from jax import lax
from jax.experimental import pallas as pl
from jax.experimental.pallas import tpu as pltpu
from jax.sharding import PartitionSpec as P

MESH = pl.DeviceIdType.MESH
LANES = 128
TILE = 256
CHUNK = 1536
highest = lax.Precision.HIGHEST
VM = pl.BlockSpec(memory_space=pltpu.VMEM)


def dot(a, b, ca, cb, precision=None):
    return lax.dot_general(
        a, b, (((ca,), (cb,)), ((), ())), precision=precision, preferred_element_type=jnp.float32
    )


def project_kernel(gx, gy, basis_ref, snap_ref, deriv_ref, pairs_ref, pen_ref,
                   rates_ref, kernel_ref, dhi_ref, dlo_ref, weights_ref,
                   part, near, mine, got, full, index_ref, sems):
    pairs = gx * gy // 2
    flat = lax.axis_index("gx") * gy + lax.axis_index("gy")
    side, spot = lax.rem(flat, 2), flat // 2
    order = basis_ref.shape[0]
    count = pairs_ref.shape[1]
    padded = dhi_ref.shape[1]

    def device(number):
        return (number // gy, lax.rem(number, gy))

    def other(k):
        return lax.rem(spot + k, pairs)

    mate = device(flat + 1 - 2 * side)
    barrier = pltpu.get_barrier_semaphore()

    def greet(k, c):
        pl.semaphore_signal(barrier, inc=1, device_id=device(other(k) * 2 + side), device_id_type=MESH)
        return c

    pl.semaphore_signal(barrier, inc=1, device_id=mate, device_id_type=MESH)
    lax.fori_loop(1, pairs, greet, 0)

    def remote(src, dst, which, phase, k, at):
        return pltpu.make_async_remote_copy(
            src_ref=src, dst_ref=dst, send_sem=sems.at[which, phase, 0, k],
            recv_sem=sems.at[which, phase, 1, k], device_id=at, device_id_type=MESH)

    def swap(c):
        return remote(part.at[c, 1 - side], near.at[c], c, 0, 0, mate)

    def scatter(c, k):
        to = other(k)
        return remote(mine.at[c, to], got.at[c, spot], c, 1, k, device(to * 2 + side))

    def spread(c, k):
        here = full.at[c, side, spot]
        return remote(here, here, c, 2, k, device(other(k) * 2 + side))

    def relay(c):
        here = full.at[c, side]
        return remote(here, here, c, 3, 0, mate)

    def each(make, c, act):
        def go(k, carry):
            getattr(make(c, k), act)()
            return carry
        lax.fori_loop(1, pairs, go, 0)

    basis = basis_ref[...]

    def project(c, ref):
        prod = dot(basis, ref[...], 1, 0)
        prod = jnp.concatenate([prod, jnp.zeros((LANES - order, prod.shape[1]), jnp.float32)], axis=0)
        for h in range(2):
            part[c, h] = prod[:, h * LANES:(h + 1) * LANES].reshape(part.shape[2:])

    def share(c):
        swap(c).wait()
        total = part[c, side] + near[c]
        mine[c] = total
        each(scatter, c, "start")
        got[c, spot] = mine[c, spot]

    def collect(c):
        each(scatter, c, "wait")
        full[c, side, spot] = jnp.sum(got[c], axis=0)
        each(spread, c, "start")

    def whole(c):
        return jnp.concatenate([full[c, h].reshape(LANES, LANES) for h in range(2)], axis=1)

    project(0, snap_ref)
    pl.semaphore_wait(barrier, pairs)
    swap(0).start()
    project(1, deriv_ref)
    swap(1).start()
    share(0)
    share(1)

    linear = lax.broadcasted_iota(jnp.int32, (2, 1 + order), 1) - 1
    fixed = jnp.where((lax.broadcasted_iota(jnp.int32, (2, 1 + order), 0) == 0) & (linear >= 0), linear, order)
    tail = jnp.full((2, padded - 1 - order - count), LANES - 1, jnp.int32)
    index_ref[...] = jnp.concatenate([fixed, pairs_ref[...], tail], axis=1)
    weights_ref[...] = jnp.zeros_like(weights_ref)
    weights_ref[0:1, 0:1 + order + count] = pen_ref[...][None, :]

    collect(0)
    collect(1)
    each(spread, 0, "wait")
    relay(0).start()
    relay(0).wait()
    coeffs = whole(0)
    ct = coeffs.T
    table = jnp.where(lax.broadcasted_iota(jnp.int32, ct.shape, 1) == order, 1.0, ct)
    t_hi = table.astype(jnp.bfloat16)
    table2 = jnp.concatenate([t_hi, (table - t_hi.astype(jnp.float32)).astype(jnp.bfloat16)], axis=1)
    io = lax.broadcasted_iota(jnp.int32, (LANES, TILE), 0)
    each(spread, 1, "wait")
    relay(1).start()

    def pick_mxu(row):
        hot = jnp.where(io == row, 1.0, 0.0).astype(jnp.bfloat16)
        return dot(table2, jnp.concatenate([hot, hot], axis=0), 1, 0)

    def pick_xlu(row):
        return jnp.concatenate([jnp.take_along_axis(
            table, jnp.broadcast_to(row[:, h:h + LANES], table.shape), axis=1, mode="promise_in_bounds")
            for h in range(0, TILE, LANES)], axis=1)

    def build(at, carry):
        for u in range(CHUNK // TILE):
            sl = pl.ds(pl.multiple_of(at * CHUNK + u * TILE, TILE), TILE)
            d = pick_xlu(index_ref[0:1, sl]) * pick_mxu(index_ref[1:2, sl])
            d_hi = d.astype(jnp.bfloat16)
            dhi_ref[:, sl] = d_hi
            dlo_ref[:, sl] = (d - d_hi.astype(jnp.float32)).astype(jnp.bfloat16)
        return carry

    lax.fori_loop(0, padded // CHUNK, build, 0)
    inner = dot(ct, coeffs, 1, 0, highest)
    sq = coeffs * coeffs
    kernel_ref[...] = 1.0 + inner + 0.5 * (inner * inner + dot(ct * ct, sq, 1, 0, highest))
    relay(1).wait()
    rates_ref[...] = whole(1)[:order]


def fit_kernel(rates_ref, kernel_ref, dhi_ref, dlo_ref, pen_ref, out_ref, t_ref, w_ref, x_ref, pt_ref, sem):
    order, snaps = rates_ref.shape
    padded = t_ref.shape[1]
    width = x_ref.shape[1]
    g = rates_ref[...] * (1.0 / math.sqrt(snaps))
    kernel = kernel_ref[...]
    s1 = dot(g, kernel, 1, 0, highest)
    lhs = jnp.concatenate([g, s1 * (1.0 / snaps)], axis=0)
    lhs_hi = lhs.astype(jnp.bfloat16)
    lhs_lo = (lhs - lhs_hi.astype(jnp.float32)).astype(jnp.bfloat16)
    lhs_both = jnp.concatenate([lhs_hi, lhs_lo], axis=0)

    def tile(at, carry):
        tt, tw = carry
        for u in range(CHUNK // TILE):
            sl = pl.ds(pl.multiple_of(at * CHUNK + u * TILE, TILE), TILE)
            both = dot(lhs_both, dhi_ref[:, sl], 1, 0)
            tv = both[:2 * order] + both[2 * order:] + dot(lhs_hi, dlo_ref[:, sl], 1, 0)
            t, v = tv[:order], tv[order:]
            pt = pen_ref[0:1, sl] * t
            w = v + pt
            t_ref[:, sl] = t
            w_ref[:, sl] = w
            pt_ref[:, sl] = pt.astype(jnp.bfloat16)
            sq, cross = t * t, t * w
            for h in range(0, TILE, LANES):
                tt = tt + sq[:, h:h + LANES]
                tw = tw + cross[:, h:h + LANES]
        return tt, tw

    zero = jnp.zeros((order, LANES), jnp.float32)
    tt, tw = lax.fori_loop(0, padded // CHUNK, tile, (zero, zero))
    dpt = dot(dhi_ref[...], pt_ref[...], 1, 1)
    tt = jnp.sum(tt, axis=1, keepdims=True)
    tw = jnp.sum(tw, axis=1, keepdims=True)
    alpha = tt / tw
    ks1 = dot(s1, kernel, 1, 0, highest) * (1.0 / snaps)
    image = ks1 + jnp.pad(dpt, ((0, 0), (0, LANES - order))).T[:order]
    moved = s1 - alpha * image
    gram = jnp.sum(moved * moved, axis=1, keepdims=True) * (1.0 / snaps)
    group = 8 * max(d for d in range(1, 6) if order // 8 % d == 0)
    copies = []
    for at in range(0, order, group):
        rows = slice(at, at + group)
        a = alpha[rows]
        t, w = t_ref[rows, :], w_ref[rows, :]
        r = t - a * w
        rr = r * r
        weighted = jnp.sum(rr * pen_ref[0:1, :], axis=1, keepdims=True) + gram[rows]
        now = jnp.sum(rr, axis=1, keepdims=True)
        ratio = now / tt[rows]
        second = now / (weighted - ratio * now / a)
        x = (a + second * ratio) * t + second * r
        x_ref[rows, :] = x[:, :width]
        copy = pltpu.make_async_copy(x_ref.at[rows, :], out_ref.at[rows, :], sem.at[at // group])
        copy.start()
        copies.append(copy)
    for copy in copies:
        copy.wait()


def solution(mesh):
    gx, gy = mesh.shape["gx"], mesh.shape["gy"]
    pairs = gx * gy // 2

    def on_device(basis, snapshots, derivatives, quad_pairs, penalty):
        order, snaps = basis.shape[1], snapshots.shape[1]
        width = 1 + order + quad_pairs.shape[1]
        padded = -(-width // CHUNK) * CHUNK
        f32, bf16 = jnp.float32, jnp.bfloat16
        block = (pairs, LANES // pairs, LANES)
        rates, kernel, dhi, dlo, weights = pl.pallas_call(
            functools.partial(project_kernel, gx, gy),
            out_shape=[
                jax.ShapeDtypeStruct((order, snaps), f32),
                jax.ShapeDtypeStruct((snaps, snaps), f32),
                jax.ShapeDtypeStruct((snaps, padded), bf16),
                jax.ShapeDtypeStruct((snaps, padded), bf16),
                jax.ShapeDtypeStruct((1, padded), f32),
            ],
            in_specs=[VM] * 5,
            out_specs=[VM] * 5,
            scratch_shapes=[
                pltpu.VMEM((2, 2) + block, f32),
                pltpu.VMEM((2,) + block, f32),
                pltpu.VMEM((2,) + block, f32),
                pltpu.VMEM((2,) + block, f32),
                pltpu.VMEM((2, 2) + block, f32),
                pltpu.VMEM((2, padded), jnp.int32),
                pltpu.SemaphoreType.DMA((2, 4, 2, pairs)),
            ],
            compiler_params=pltpu.CompilerParams(
                collective_id=0, has_side_effects=True, vmem_limit_bytes=24 * 1024 * 1024),
            name="project",
        )(basis.T, snapshots, derivatives, quad_pairs, penalty)
        return pl.pallas_call(
            fit_kernel,
            out_shape=jax.ShapeDtypeStruct((order, width), f32),
            in_specs=[VM] * 5,
            out_specs=pl.BlockSpec(memory_space=pl.ANY),
            scratch_shapes=[
                pltpu.VMEM((order, padded), f32),
                pltpu.VMEM((order, padded), f32),
                pltpu.VMEM((order, width), f32),
                pltpu.VMEM((order, padded), bf16),
                pltpu.SemaphoreType.DMA((order // 8,)),
            ],
            compiler_params=pltpu.CompilerParams(vmem_limit_bytes=24 * 1024 * 1024),
            name="fit",
        )(rates, kernel, dhi, dlo, weights)

    in_specs = (P(("gx", "gy"), None), P(("gx", "gy"), None), P(("gx", "gy"), None), P(), P())
    return jax.shard_map(on_device, mesh=mesh, in_specs=in_specs, out_specs=P(), check_vma=False)
```

time: 57.6 us -> 38.6 us (0.67)
  Pallas kernels: 52.2 us -> 33.5 us
    pallas_call x2, Pallas kernels: 52.2 us -> 33.5 us  [the longest x1 24.8 us: on_device(): pl.pallas_call(functools.partial(project_kernel, gx, gy), out_shape=[jax....]
    unnamed x3 -> x10, local copies, waits for them, and re-layouts: 2.81 us -> 4.72 us
    slice x1 -> x0, local copies, waits for them, and re-layouts: 1.04 us -> none  [on_device(): quad_pairs[0]]
    pad x1 -> x0, local copies, waits for them, and re-layouts: 0.76 us -> none  [on_device(): weights = jnp.pad(penalty, (0, padded - width))[None, :]]
where the time goes in v1:
time: 38.6 us; the launch traced here: 38.3 us
  Pallas kernels  33.5 us (87%)
  local copies, waits for them, and re-layouts  4.72 us (12%)
    pallas_call x1, Pallas kernels, on_device(): pl.pallas_call(functools.partial(project_kernel, gx, gy), out_shape=[jax....  24.8 us
    pallas_call x1, Pallas kernels, on_device(): pl.pallas_call(fit_kernel, out_shape=jax.ShapeDtypeStruct((order, width),...  8.68 us
    unnamed x10, local copies, waits for them, and re-layouts  4.72 us

profile of v1, /device:TPU:0, one launch (start us, length us, event | category | flops | bytes accessed | tf_op | source)
XLA Modules:
  0.0 38.3 jit_solution(9749703412378229198)
XLA Ops:
  0.0 0.0 copy-start
  0.0 1.1 %copy-done = bf16[1280,256]{1,0:T(8,128)(2,1)S(1)} copy-done((bf16[1280,256]{1,0:T(8,128)(2,1)S(1)}, bf16[1280,256]{1,0:T(8,128)(2,1)}, u32[]{:S(2)}) %copy-start) | copy-done | bytes 655384
  1.1 0.0 copy-start.1
  1.1 1.1 %copy-done.1 = bf16[1280,256]{1,0:T(8,128)(2,1)S(1)} copy-done((bf16[1280,256]{1,0:T(8,128)(2,1)S(1)}, bf16[1280,256]{1,0:T(8,128)(2,1)}, u32[]{:S(2)}) %copy-start.1) | copy-done | bytes 655384
  2.2 0.0 copy-start.2
  2.2 1.0 %copy-done.2 = bf16[1280,120]{0,1:T(8,128)(2,1)S(1)} copy-done((bf16[1280,120]{0,1:T(8,128)(2,1)S(1)}, bf16[1280,120]{0,1:T(8,128)(2,1)}, u32[]{:S(2)}) %copy-start.2) | copy-done | bytes 307224
  3.1 0.0 copy-start.3
  3.1 0.8 %copy-done.3 = s32[2,7260]{1,0:T(2,128)S(1)} copy-done((s32[2,7260]{1,0:T(2,128)S(1)}, s32[2,7260]{1,0:T(2,128)}, u32[]{:S(2)}) %copy-start.3) | copy-done | bytes 58104
  4.0 0.0 copy-start.4
  4.0 0.8 %copy-done.4 = f32[7381]{0:T(1024)S(1)} copy-done((f32[7381]{0:T(1024)S(1)}, f32[7381]{0:T(1024)}, u32[]{:S(2)}) %copy-start.4) | copy-done | bytes 29548
  4.7 24.8 %project.1 = (f32[120,256]{1,0:T(8,128)S(1)}, f32[256,256]{1,0:T(8,128)S(1)}, bf16[256,7680]{1,0:T(8,128)(2,1)S(1)}, bf16[256,7680]{1,0:T(8,128)(2,1)S(1)}, f32[1,7680]{1,0:T(1,128)S(1)}) custom-call(bf16[120,1280]{1,0:T(8,128)(2,1)S(1)} %bitcast.1, bf16[1280,256]{1,0:T(8,128)(2,1)S(1)} %copy-done, bf16[1280,256]{1,0:T(8,128)(2,1)S(1)} %copy-done.1, ...), custom_call_target="tpu_custom_call" | custom-call | tf_op jit(solution)/shard_map/project/pallas_call | solution.py:226
  29.6 8.7 %fit.1 = f32[120,7381]{1,0:T(8,128)} custom-call(f32[120,256]{1,0:T(8,128)S(1)} %get-tuple-element.10.rates_ref, f32[256,256]{1,0:T(8,128)S(1)} %get-tuple-element.11.kernel_ref, bf16[256,7680]{1,0:T(8,128)(2,1)S(1)} %get-tuple-element.12.dhi_ref, bf16[256,7680]{1,0:T(8,128)(2,1)S(1)} %get-tuple-element.13.dlo_ref, f32[1,7680]{1,0:T(1,128)S(1)} %get-tuple-element.14.pen_ref), custom_call_target="tpu_custom_call" | custom-call | tf_op jit(solution)/shard_map/fit/pallas_call | solution.py:250
Async XLA Ops:
  0.0 1.1 %copy-start = (bf16[1280,256]{1,0:T(8,128)(2,1)S(1)}, bf16[1280,256]{1,0:T(8,128)(2,1)}, u32[]{:S(2)}) copy-start(bf16[1280,256]{1,0:T(8,128)(2,1)} %snap_ref.1) | copy-start | bytes 1966084
  1.1 1.1 %copy-start.1 = (bf16[1280,256]{1,0:T(8,128)(2,1)S(1)}, bf16[1280,256]{1,0:T(8,128)(2,1)}, u32[]{:S(2)}) copy-start(bf16[1280,256]{1,0:T(8,128)(2,1)} %deriv_ref.1) | copy-start | bytes 1966084
  2.2 1.0 %copy-start.2 = (bf16[1280,120]{0,1:T(8,128)(2,1)S(1)}, bf16[1280,120]{0,1:T(8,128)(2,1)}, u32[]{:S(2)}) copy-start(bf16[1280,120]{0,1:T(8,128)(2,1)} %param.5) | copy-start | bytes 921604
  3.1 0.8 %copy-start.3 = (s32[2,7260]{1,0:T(2,128)S(1)}, s32[2,7260]{1,0:T(2,128)}, u32[]{:S(2)}) copy-start(s32[2,7260]{1,0:T(2,128)} %pairs_ref.1) | copy-start | bytes 174244
  4.0 0.8 %copy-start.4 = (f32[7381]{0:T(1024)S(1)}, f32[7381]{0:T(1024)}, u32[]{:S(2)}) copy-start(f32[7381]{0:T(1024)} %pen_ref.1) | copy-start | bytes 88576

commit v2 on v1

--- a/solution.py
+++ b/solution.py
@@ -14,6 +14,7 @@
 CHUNK = 1536
 highest = lax.Precision.HIGHEST
 VM = pl.BlockSpec(memory_space=pltpu.VMEM)
+HBM = pl.BlockSpec(memory_space=pltpu.HBM)
 
 
 def dot(a, b, ca, cb, precision=None):
@@ -22,9 +23,10 @@
     )
 
 
-def project_kernel(gx, gy, basis_ref, snap_ref, deriv_ref, pairs_ref, pen_ref,
+def project_kernel(gx, gy, basis_hbm, snap_hbm, deriv_hbm, pairs_hbm, pen_hbm,
                    rates_ref, kernel_ref, dhi_ref, dlo_ref, weights_ref,
-                   part, near, mine, got, full, index_ref, sems):
+                   basis_ref, snap_ref, deriv_ref, pairs_ref, pen_ref,
+                   part, near, mine, got, full, hot_i, hot_j, load_sems, sems):
     pairs = gx * gy // 2
     flat = lax.axis_index("gx") * gy + lax.axis_index("gy")
     side, spot = lax.rem(flat, 2), flat // 2
@@ -47,6 +49,14 @@
 
     pl.semaphore_signal(barrier, inc=1, device_id=mate, device_id_type=MESH)
     lax.fori_loop(1, pairs, greet, 0)
+    loads = [
+        pltpu.make_async_copy(src, dst, load_sems.at[k])
+        for k, (src, dst) in enumerate((
+            (basis_hbm, basis_ref), (snap_hbm, snap_ref), (deriv_hbm, deriv_ref),
+            (pairs_hbm, pairs_ref), (pen_hbm, pen_ref)))
+    ]
+    for load in loads:
+        load.start()
 
     def remote(src, dst, which, phase, k, at):
         return pltpu.make_async_remote_copy(
@@ -74,10 +84,8 @@
             return carry
         lax.fori_loop(1, pairs, go, 0)
 
-    basis = basis_ref[...]
-
     def project(c, ref):
-        prod = dot(basis, ref[...], 1, 0)
+        prod = dot(basis_ref[...], ref[...], 1, 0)
         prod = jnp.concatenate([prod, jnp.zeros((LANES - order, prod.shape[1]), jnp.float32)], axis=0)
         for h in range(2):
             part[c, h] = prod[:, h * LANES:(h + 1) * LANES].reshape(part.shape[2:])
@@ -97,54 +105,62 @@
     def whole(c):
         return jnp.concatenate([full[c, h].reshape(LANES, LANES) for h in range(2)], axis=1)
 
+    loads[0].wait()
+    loads[1].wait()
     project(0, snap_ref)
     pl.semaphore_wait(barrier, pairs)
     swap(0).start()
+    loads[2].wait()
     project(1, deriv_ref)
     swap(1).start()
     share(0)
     share(1)
 
+    loads[3].wait()
+    loads[4].wait()
     linear = lax.broadcasted_iota(jnp.int32, (2, 1 + order), 1) - 1
     fixed = jnp.where((lax.broadcasted_iota(jnp.int32, (2, 1 + order), 0) == 0) & (linear >= 0), linear, order)
     tail = jnp.full((2, padded - 1 - order - count), LANES - 1, jnp.int32)
-    index_ref[...] = jnp.concatenate([fixed, pairs_ref[...], tail], axis=1)
+    index = jnp.concatenate([fixed, pairs_ref[...], tail], axis=1)
+    io = lax.broadcasted_iota(jnp.int32, (LANES, padded), 0)
+    hot_i[...] = jnp.where(io == index[0:1], 1.0, 0.0).astype(jnp.bfloat16)
+    hot_j[...] = jnp.where(io == index[1:2], 1.0, 0.0).astype(jnp.bfloat16)
     weights_ref[...] = jnp.zeros_like(weights_ref)
     weights_ref[0:1, 0:1 + order + count] = pen_ref[...][None, :]
+
+    def build(h):
+        table = full[0, h].reshape(LANES, LANES).T
+        table = jnp.where(lax.broadcasted_iota(jnp.int32, table.shape, 1) == order, 1.0, table)
+        t_hi = table.astype(jnp.bfloat16)
+        both = jnp.concatenate([t_hi, (table - t_hi.astype(jnp.float32)).astype(jnp.bfloat16)], axis=1)
+        rows = pl.ds(pl.multiple_of(h * LANES, LANES), LANES)
+
+        def pick(ref, sl):
+            hot = ref[:, sl]
+            return dot(both, jnp.concatenate([hot, hot], axis=0), 1, 0)
+
+        def step(at, carry):
+            for u in range(CHUNK // TILE):
+                sl = pl.ds(pl.multiple_of(at * CHUNK + u * TILE, TILE), TILE)
+                d = pick(hot_i, sl) * pick(hot_j, sl)
+                d_hi = d.astype(jnp.bfloat16)
+                dhi_ref[rows, sl] = d_hi
+                dlo_ref[rows, sl] = (d - d_hi.astype(jnp.float32)).astype(jnp.bfloat16)
+            return carry
+
+        lax.fori_loop(0, padded // CHUNK, step, 0)
 
     collect(0)
     collect(1)
     each(spread, 0, "wait")
     relay(0).start()
+    build(side)
     relay(0).wait()
+    each(spread, 1, "wait")
+    relay(1).start()
+    build(1 - side)
     coeffs = whole(0)
     ct = coeffs.T
-    table = jnp.where(lax.broadcasted_iota(jnp.int32, ct.shape, 1) == order, 1.0, ct)
-    t_hi = table.astype(jnp.bfloat16)
-    table2 = jnp.concatenate([t_hi, (table - t_hi.astype(jnp.float32)).astype(jnp.bfloat16)], axis=1)
-    io = lax.broadcasted_iota(jnp.int32, (LANES, TILE), 0)
-    each(spread, 1, "wait")
-    relay(1).start()
-
-    def pick_mxu(row):
-        hot = jnp.where(io == row, 1.0, 0.0).astype(jnp.bfloat16)
-        return dot(table2, jnp.concatenate([hot, hot], axis=0), 1, 0)
-
-    def pick_xlu(row):
-        return jnp.concatenate([jnp.take_along_axis(
-            table, jnp.broadcast_to(row[:, h:h + LANES], table.shape), axis=1, mode="promise_in_bounds")
-            for h in range(0, TILE, LANES)], axis=1)
-
-    def build(at, carry):
-        for u in range(CHUNK // TILE):
-            sl = pl.ds(pl.multiple_of(at * CHUNK + u * TILE, TILE), TILE)
-            d = pick_xlu(index_ref[0:1, sl]) * pick_mxu(index_ref[1:2, sl])
-            d_hi = d.astype(jnp.bfloat16)
-            dhi_ref[:, sl] = d_hi
-            dlo_ref[:, sl] = (d - d_hi.astype(jnp.float32)).astype(jnp.bfloat16)
-        return carry
-
-    lax.fori_loop(0, padded // CHUNK, build, 0)
     inner = dot(ct, coeffs, 1, 0, highest)
     sq = coeffs * coeffs
     kernel_ref[...] = 1.0 + inner + 0.5 * (inner * inner + dot(ct * ct, sq, 1, 0, highest))
@@ -232,21 +248,28 @@
                 jax.ShapeDtypeStruct((snaps, padded), bf16),
                 jax.ShapeDtypeStruct((1, padded), f32),
             ],
-            in_specs=[VM] * 5,
+            in_specs=[HBM] * 5,
             out_specs=[VM] * 5,
             scratch_shapes=[
+                pltpu.VMEM((order, basis.shape[0]), bf16),
+                pltpu.VMEM(snapshots.shape, bf16),
+                pltpu.VMEM(derivatives.shape, bf16),
+                pltpu.VMEM(quad_pairs.shape, jnp.int32),
+                pltpu.VMEM(penalty.shape, f32),
                 pltpu.VMEM((2, 2) + block, f32),
                 pltpu.VMEM((2,) + block, f32),
                 pltpu.VMEM((2,) + block, f32),
                 pltpu.VMEM((2,) + block, f32),
                 pltpu.VMEM((2, 2) + block, f32),
-                pltpu.VMEM((2, padded), jnp.int32),
+                pltpu.VMEM((LANES, padded), bf16),
+                pltpu.VMEM((LANES, padded), bf16),
+                pltpu.SemaphoreType.DMA((5,)),
                 pltpu.SemaphoreType.DMA((2, 4, 2, pairs)),
             ],
             compiler_params=pltpu.CompilerParams(
                 collective_id=0, has_side_effects=True, vmem_limit_bytes=24 * 1024 * 1024),
             name="project",
-        )(basis.T, snapshots, derivatives, quad_pairs, penalty)
+        )(*(pltpu.with_memory_space_constraint(v, pltpu.HBM) for v in (basis.T, snapshots, derivatives, quad_pairs, penalty)))
         return pl.pallas_call(
             fit_kernel,
             out_shape=jax.ShapeDtypeStruct((order, width), f32),

time: 38.6 us -> 33.9 us (0.88)
  local copies, waits for them, and re-layouts: 4.72 us -> 0 us
    unnamed x10 -> x0, local copies, waits for them, and re-layouts: 4.72 us -> none
where the time goes in v2:
time: 33.9 us; the launch traced here: 33.7 us
  Pallas kernels  33.7 us (99%)
    pallas_call x1, Pallas kernels, on_device(): pl.pallas_call(functools.partial(project_kernel, gx, gy), out_shape=[jax....  25 us
    pallas_call x1, Pallas kernels, on_device(): pl.pallas_call(fit_kernel, out_shape=jax.ShapeDtypeStruct((order, width),...  8.75 us

profile of v2, /device:TPU:0, one launch (start us, length us, event | category | flops | bytes accessed | tf_op | source)
XLA Modules:
  0.0 33.7 jit_solution(17435407244078857380)
XLA Ops:
  0.0 25.0 %project.1 = (f32[120,256]{1,0:T(8,128)S(1)}, f32[256,256]{1,0:T(8,128)S(1)}, bf16[256,7680]{1,0:T(8,128)(2,1)S(1)}, bf16[256,7680]{1,0:T(8,128)(2,1)S(1)}, f32[1,7680]{1,0:T(1,128)S(1)}) custom-call(bf16[120,1280]{1,0:T(8,128)(2,1)} %bitcast.1, bf16[1280,256]{1,0:T(8,128)(2,1)} %snap_hbm.1, bf16[1280,256]{1,0:T(8,128)(2,1)} %deriv_hbm.1, ...), custom_call_target="tpu_custom_call" | custom-call | tf_op jit(solution)/shard_map/project/pallas_call | solution.py:242
  25.0 8.8 %fit.1 = f32[120,7381]{1,0:T(8,128)} custom-call(f32[120,256]{1,0:T(8,128)S(1)} %get-tuple-element.10.rates_ref, f32[256,256]{1,0:T(8,128)S(1)} %get-tuple-element.11.kernel_ref, bf16[256,7680]{1,0:T(8,128)(2,1)S(1)} %get-tuple-element.12.dhi_ref, bf16[256,7680]{1,0:T(8,128)(2,1)S(1)} %get-tuple-element.13.dlo_ref, f32[1,7680]{1,0:T(1,128)S(1)} %get-tuple-element.14.pen_ref), custom_call_target="tpu_custom_call" | custom-call | tf_op jit(solution)/shard_map/fit/pallas_call | solution.py:273

commit v3 on v2

--- a/solution.py
+++ b/solution.py
@@ -11,8 +11,8 @@
 MESH = pl.DeviceIdType.MESH
 LANES = 128
 TILE = 256
-CHUNK = 1536
-highest = lax.Precision.HIGHEST
+CHUNK = 3840
+highest = lax.Precision.HIGH
 VM = pl.BlockSpec(memory_space=pltpu.VMEM)
 HBM = pl.BlockSpec(memory_space=pltpu.HBM)
 
@@ -78,8 +78,11 @@
         here = full.at[c, side]
         return remote(here, here, c, 3, 0, mate)
 
+    upper = spot // (pairs // 2)
+
     def each(make, c, act):
-        def go(k, carry):
+        def go(j, carry):
+            k = upper * j + (1 - upper) * (pairs - j)
             getattr(make(c, k), act)()
             return carry
         lax.fori_loop(1, pairs, go, 0)
@@ -208,7 +211,7 @@
     image = ks1 + jnp.pad(dpt, ((0, 0), (0, LANES - order))).T[:order]
     moved = s1 - alpha * image
     gram = jnp.sum(moved * moved, axis=1, keepdims=True) * (1.0 / snaps)
-    group = 8 * max(d for d in range(1, 6) if order // 8 % d == 0)
+    group = 8 * max(d for d in range(1, 4) if order // 8 % d == 0)
     copies = []
     for at in range(0, order, group):
         rows = slice(at, at + group)
@@ -220,7 +223,7 @@
         now = jnp.sum(rr, axis=1, keepdims=True)
         ratio = now / tt[rows]
         second = now / (weighted - ratio * now / a)
-        x = (a + second * ratio) * t + second * r
+        x = (a + second * ratio + second) * t - (second * a) * w
         x_ref[rows, :] = x[:, :width]
         copy = pltpu.make_async_copy(x_ref.at[rows, :], out_ref.at[rows, :], sem.at[at // group])
         copy.start()

time: 33.9 us -> 30.7 us (0.906)
  Pallas kernels: 33.7 us -> 30.6 us
    pallas_call x1, Pallas kernels: 25 us -> 22.7 us  [on_device(): pl.pallas_call(functools.partial(project_kernel, gx, gy), out_shape=[jax....]
    pallas_call x1, Pallas kernels: 8.75 us -> 7.88 us  [on_device(): pl.pallas_call(fit_kernel, out_shape=jax.ShapeDtypeStruct((order, width),...]
where the time goes in v3:
time: 30.7 us; the launch traced here: 30.6 us
  Pallas kernels  30.6 us (100%)
    pallas_call x1, Pallas kernels, on_device(): pl.pallas_call(functools.partial(project_kernel, gx, gy), out_shape=[jax....  22.7 us
    pallas_call x1, Pallas kernels, on_device(): pl.pallas_call(fit_kernel, out_shape=jax.ShapeDtypeStruct((order, width),...  7.88 us

profile of v3, /device:TPU:0, one launch (start us, length us, event | category | flops | bytes accessed | tf_op | source)
XLA Modules:
  0.0 30.6 jit_solution(10898844367059543069)
XLA Ops:
  0.0 22.7 %project.1 = (f32[120,256]{1,0:T(8,128)S(1)}, f32[256,256]{1,0:T(8,128)S(1)}, bf16[256,7680]{1,0:T(8,128)(2,1)S(1)}, bf16[256,7680]{1,0:T(8,128)(2,1)S(1)}, f32[1,7680]{1,0:T(1,128)S(1)}) custom-call(bf16[120,1280]{1,0:T(8,128)(2,1)} %bitcast.1, bf16[1280,256]{1,0:T(8,128)(2,1)} %snap_hbm.1, bf16[1280,256]{1,0:T(8,128)(2,1)} %deriv_hbm.1, ...), custom_call_target="tpu_custom_call" | custom-call | tf_op jit(solution)/shard_map/project/pallas_call | solution.py:245
  22.7 7.9 %fit.1 = f32[120,7381]{1,0:T(8,128)} custom-call(f32[120,256]{1,0:T(8,128)S(1)} %get-tuple-element.10.rates_ref, f32[256,256]{1,0:T(8,128)S(1)} %get-tuple-element.11.kernel_ref, bf16[256,7680]{1,0:T(8,128)(2,1)S(1)} %get-tuple-element.12.dhi_ref, bf16[256,7680]{1,0:T(8,128)(2,1)S(1)} %get-tuple-element.13.dlo_ref, f32[1,7680]{1,0:T(1,128)S(1)} %get-tuple-element.14.pen_ref), custom_call_target="tpu_custom_call" | custom-call | tf_op jit(solution)/shard_map/fit/pallas_call | solution.py:276

commit v4 on v3

--- a/solution.py
+++ b/solution.py
@@ -11,7 +11,7 @@
 MESH = pl.DeviceIdType.MESH
 LANES = 128
 TILE = 256
-CHUNK = 3840
+CHUNK = 7680
 highest = lax.Precision.HIGH
 VM = pl.BlockSpec(memory_space=pltpu.VMEM)
 HBM = pl.BlockSpec(memory_space=pltpu.HBM)
@@ -144,14 +144,15 @@
 
         def step(at, carry):
             for u in range(CHUNK // TILE):
-                sl = pl.ds(pl.multiple_of(at * CHUNK + u * TILE, TILE), TILE)
+                sl = pl.ds(at * CHUNK + u * TILE, TILE)
                 d = pick(hot_i, sl) * pick(hot_j, sl)
                 d_hi = d.astype(jnp.bfloat16)
                 dhi_ref[rows, sl] = d_hi
                 dlo_ref[rows, sl] = (d - d_hi.astype(jnp.float32)).astype(jnp.bfloat16)
             return carry
 
-        lax.fori_loop(0, padded // CHUNK, step, 0)
+        for at in range(padded // CHUNK):
+            step(at, 0)
 
     collect(0)
     collect(1)
@@ -186,7 +187,7 @@
     def tile(at, carry):
         tt, tw = carry
         for u in range(CHUNK // TILE):
-            sl = pl.ds(pl.multiple_of(at * CHUNK + u * TILE, TILE), TILE)
+            sl = pl.ds(at * CHUNK + u * TILE, TILE)
             both = dot(lhs_both, dhi_ref[:, sl], 1, 0)
             tv = both[:2 * order] + both[2 * order:] + dot(lhs_hi, dlo_ref[:, sl], 1, 0)
             t, v = tv[:order], tv[order:]
@@ -202,7 +203,9 @@
         return tt, tw
 
     zero = jnp.zeros((order, LANES), jnp.float32)
-    tt, tw = lax.fori_loop(0, padded // CHUNK, tile, (zero, zero))
+    tt, tw = zero, zero
+    for at in range(padded // CHUNK):
+        tt, tw = tile(at, (tt, tw))
     dpt = dot(dhi_ref[...], pt_ref[...], 1, 1)
     tt = jnp.sum(tt, axis=1, keepdims=True)
     tw = jnp.sum(tw, axis=1, keepdims=True)

time: 30.7 us -> 29.9 us (0.974)
  Pallas kernels: 30.6 us -> 29.8 us
    pallas_call x1, Pallas kernels: 22.7 us -> 22 us  [on_device(): pl.pallas_call(functools.partial(project_kernel, gx, gy), out_shape=[jax....]
where the time goes in v4:
time: 29.9 us; the launch traced here: 29.8 us
  Pallas kernels  29.8 us (100%)
    pallas_call x1, Pallas kernels, on_device(): pl.pallas_call(functools.partial(project_kernel, gx, gy), out_shape=[jax....  22 us
    pallas_call x1, Pallas kernels, on_device(): pl.pallas_call(fit_kernel, out_shape=jax.ShapeDtypeStruct((order, width),...  7.78 us

profile of v4, /device:TPU:0, one launch (start us, length us, event | category | flops | bytes accessed | tf_op | source)
XLA Modules:
  0.0 29.8 jit_solution(6836517128645579161)
XLA Ops:
  0.0 22.0 %project.1 = (f32[120,256]{1,0:T(8,128)S(1)}, f32[256,256]{1,0:T(8,128)S(1)}, bf16[256,7680]{1,0:T(8,128)(2,1)S(1)}, bf16[256,7680]{1,0:T(8,128)(2,1)S(1)}, f32[1,7680]{1,0:T(1,128)S(1)}) custom-call(bf16[120,1280]{1,0:T(8,128)(2,1)} %bitcast.1, bf16[1280,256]{1,0:T(8,128)(2,1)} %snap_hbm.1, bf16[1280,256]{1,0:T(8,128)(2,1)} %deriv_hbm.1, ...), custom_call_target="tpu_custom_call" | custom-call | tf_op jit(solution)/shard_map/project/pallas_call | solution.py:248
  22.0 7.8 %fit.1 = f32[120,7381]{1,0:T(8,128)} custom-call(f32[120,256]{1,0:T(8,128)S(1)} %get-tuple-element.10.rates_ref, f32[256,256]{1,0:T(8,128)S(1)} %get-tuple-element.11.kernel_ref, bf16[256,7680]{1,0:T(8,128)(2,1)S(1)} %get-tuple-element.12.dhi_ref, bf16[256,7680]{1,0:T(8,128)(2,1)S(1)} %get-tuple-element.13.dlo_ref, f32[1,7680]{1,0:T(1,128)S(1)} %get-tuple-element.14.pen_ref), custom_call_target="tpu_custom_call" | custom-call | tf_op jit(solution)/shard_map/fit/pallas_call | solution.py:279
